TPU v7x, 32 devices: a whole 2x2x4 slice. The times are simulated.
32 devices in a mesh: dp: 8 (over z, y), tensor: 4 (over x, core).
Axes of the slice: x: 2, y: 2, z: 4, core: 2. Of those that a mesh axis runs over, the one named last changes fastest.
Arguments:
- acts: bfloat16 [8, 2048, 1024], P('dp', 'tensor'), may hold values from -6 to 6
- grad_out: bfloat16 [8, 2048, 1024], P('dp', 'tensor'), may hold values from -6 to 6
- norm_gain: float32 [1024], replicated, may hold values from 0.5 to 1.5
- w_zx: bfloat16 [1024, 2, 2048], P('dp', None, 'tensor'), may hold values from -0.1875 to 0.1875
- w_bc: bfloat16 [1024, 256], P('dp'), may hold values from -0.1875 to 0.1875
- w_dt: bfloat16 [1024, 32], P('dp', 'tensor'), may hold values from -0.1875 to 0.1875
- w_out: bfloat16 [1024, 2048], P('dp', 'tensor'), may hold values from -0.125 to 0.125
- conv_x: float32 [4, 2048], replicated, may hold values from -3 to 3
- conv_x_bias: float32 [2048], replicated, may hold values from -0.5 to 0.5
- conv_bc: float32 [4, 256], replicated, may hold values from -3 to 3
- conv_bc_bias: float32 [256], replicated, may hold values from -0.5 to 0.5
- dt_bias: float32 [32], replicated, may hold values from -7 to -2
- a_log: float32 [32], replicated, may hold values from 0 to 2.77
- d_skip: float32 [32], replicated, may hold values from 0.5 to 1.5
- gate_gain: float32 [2048], replicated, may hold values from 0.5 to 1.5
Outputs:
- out_acts: bfloat16 [8, 2048, 1024], P('dp', 'tensor')
- grad_acts: float32 [8, 2048, 1024], P('dp', 'tensor')
- grad_norm_gain: float32 [1024], replicated
- grad_w_zx: float32 [1024, 2, 2048], P('dp', None, 'tensor')
- grad_w_bc: float32 [1024, 256], P('dp')
- grad_w_dt: float32 [1024, 32], P('dp', 'tensor')
- grad_w_out: float32 [1024, 2048], P('dp', 'tensor')
- grad_conv_x: float32 [4, 2048], replicated
- grad_conv_x_bias: float32 [2048], replicated
- grad_conv_bc: float32 [4, 256], replicated
- grad_conv_bc_bias: float32 [256], replicated
- grad_dt_bias: float32 [32], replicated
- grad_a_log: float32 [32], replicated
- grad_d_skip: float32 [32], replicated
- grad_gate_gain: float32 [2048], replicated
All inputs are finite; a program needn't handle non-finite values.
Results may differ from a plain program's by a relative error of at most 0.0096.
Values may be sent and summed in bfloat16 or wider, within the bound.
A program may use at most 192 MiB of HBM per device.

v0:
```python
import jax
import jax.numpy as jnp
from jax import lax
from jax.sharding import PartitionSpec as P

BLOCK_LEN = 256


EPSILON = 1e-05
FULL_PRECISION = lax.Precision.HIGHEST
CONTRACT_LAST = (((1,), (1,)), ((), ()))
CONTRACT_FIRST = (((0,), (0,)), ((), ()))


def causal_conv(values, conv_taps):
    tap_count = conv_taps.shape[0]
    length = values.shape[0]
    padded = jnp.pad(values, ((tap_count - 1, 0), (0, 0)))
    result = conv_taps[0] * padded[0:length]
    for offset in range(1, tap_count):
        result = result + conv_taps[offset] * padded[offset : offset + length]
    return result


def ssd_scan(x_heads, step_dt, decay_rate, b_mat, c_mat, block_size):
    length, head_count, head_width = x_heads.shape
    state_count = b_mat.shape[1]
    block_count = length // block_size
    x_blocks = x_heads.reshape(block_count, block_size, head_count, head_width)
    dt_blocks = step_dt.reshape(block_count, block_size, head_count)
    b_blocks = b_mat.reshape(block_count, block_size, state_count)
    c_blocks = c_mat.reshape(block_count, block_size, state_count)
    positions = jnp.arange(block_size)
    causal_mask = (positions[:, None] >= positions[None, :]).astype(jnp.float32)

    def step_block(state, inputs):
        x_block, dt_block, b_block, c_block = inputs
        cum_logs = jnp.cumsum(dt_block * decay_rate[None, :], axis=0)
        scores = jnp.dot(c_block, b_block.T, precision=FULL_PRECISION)
        log_gaps = (cum_logs[:, None, :] - cum_logs[None, :, :]) * causal_mask[:, :, None]
        weights = (
            scores[:, :, None] * jnp.exp(log_gaps) * causal_mask[:, :, None] * dt_block[None, :, :]
        )
        within = jnp.einsum("ijh,jhp->ihp", weights, x_block, precision=FULL_PRECISION)
        carried = (
            jnp.einsum("in,hpn->ihp", c_block, state, precision=FULL_PRECISION)
            * jnp.exp(cum_logs)[:, :, None]
        )
        block_total = cum_logs[-1]
        state_weight = jnp.exp(block_total[None, :] - cum_logs) * dt_block
        update = jnp.einsum(
            "jhp,jn->hpn", x_block * state_weight[:, :, None], b_block, precision=FULL_PRECISION
        )
        new_state = state * jnp.exp(block_total)[:, None, None] + update
        return (new_state, within + carried)

    zero_state = jnp.zeros((head_count, head_width, state_count), jnp.float32)
    final_state, outputs = lax.scan(
        jax.checkpoint(step_block), zero_state, (x_blocks, dt_blocks, b_blocks, c_blocks)
    )
    return outputs.reshape(length, head_count, head_width)


def pre_norm(acts_row, norm_gain):
    return (
        acts_row
        * lax.rsqrt(jnp.mean(acts_row * acts_row, axis=-1, keepdims=True) + EPSILON)
        * norm_gain
    )


def conv_part(x_vals, bc_vals, x_taps, x_shift, bc_taps, bc_shift):
    x_conv = jax.nn.silu(causal_conv(x_vals, x_taps) + x_shift)
    bc_conv = jax.nn.silu(causal_conv(bc_vals, bc_taps) + bc_shift)
    return (x_conv, bc_conv)


def mix_part(x_vals, b_vals, c_vals, dt_vals, dt_shift, log_rate, skip_gain, gate_vals):
    length = x_vals.shape[0]
    head_count = dt_vals.shape[1]
    x_heads = x_vals.reshape(length, head_count, -1)
    step_dt = jax.nn.softplus(dt_vals + dt_shift)
    mixed = (
        ssd_scan(x_heads, step_dt, -jnp.exp(log_rate), b_vals, c_vals, BLOCK_LEN)
        + skip_gain[None, :, None] * x_heads
    )
    return mixed.reshape(length, -1) * jax.nn.silu(gate_vals)


def widen(piece, start, full_size):
    holder = jnp.zeros(piece.shape[:-1] + (full_size,), jnp.float32)
    return lax.dynamic_update_slice_in_dim(holder, piece, start, piece.ndim - 1)


def body(
    acts,
    grad_out,
    norm_gain,
    w_zx,
    w_bc,
    w_dt,
    w_out,
    conv_x,
    conv_x_bias,
    conv_bc,
    conv_bc_bias,
    dt_bias,
    a_log,
    d_skip,
    gate_gain,
):
    parts = lax.axis_size("tensor")
    rank = lax.axis_index("tensor")
    local_rows = acts.shape[1]
    channels = w_zx.shape[2]
    head_count = w_dt.shape[1]
    state_count = w_bc.shape[1] // 2
    total_channels = channels * parts
    total_heads = head_count * parts
    chan_start = rank * channels
    head_start = rank * head_count
    zx_full, bc_full, dt_full, out_full = (
        lax.all_gather(w_zx, "dp", axis=0, tiled=True),
        lax.all_gather(w_bc, "dp", axis=0, tiled=True),
        lax.all_gather(w_dt, "dp", axis=0, tiled=True),
        lax.all_gather(w_out, "dp", axis=0, tiled=True),
    )
    acts_row = acts[0].astype(jnp.float32)
    normed_in, pre_back = jax.vjp(pre_norm, acts_row, norm_gain)
    hidden = lax.all_gather(normed_in.astype(jnp.bfloat16), "tensor", axis=0, tiled=True)
    zx_proj = jnp.einsum("ld,dkc->lkc", hidden, zx_full, preferred_element_type=jnp.float32)
    bc_proj = jnp.dot(hidden, bc_full, preferred_element_type=jnp.float32)
    dt_proj = jnp.dot(hidden, dt_full, preferred_element_type=jnp.float32)
    conv_x_local = lax.dynamic_slice_in_dim(conv_x, chan_start, channels, 1)
    conv_xb_local = lax.dynamic_slice_in_dim(conv_x_bias, chan_start, channels, 0)
    dt_bias_local = lax.dynamic_slice_in_dim(dt_bias, head_start, head_count, 0)
    a_log_local = lax.dynamic_slice_in_dim(a_log, head_start, head_count, 0)
    d_skip_local = lax.dynamic_slice_in_dim(d_skip, head_start, head_count, 0)
    gain_local = lax.dynamic_slice_in_dim(gate_gain, chan_start, channels, 0)
    conv_outs, conv_back = jax.vjp(
        conv_part, zx_proj[:, 1], bc_proj, conv_x_local, conv_xb_local, conv_bc, conv_bc_bias
    )
    x_conv, bc_conv = conv_outs
    x_low = x_conv.astype(jnp.bfloat16)
    b_low = bc_conv[:, :state_count].astype(jnp.bfloat16)
    c_low = bc_conv[:, state_count:].astype(jnp.bfloat16)
    gated, mix_back = jax.vjp(
        mix_part,
        x_low.astype(jnp.float32),
        b_low.astype(jnp.float32),
        c_low.astype(jnp.float32),
        dt_proj,
        dt_bias_local,
        a_log_local,
        d_skip_local,
        zx_proj[:, 0],
    )
    square_total = lax.psum(jnp.sum(gated * gated, axis=1), "tensor")
    inv_rms = lax.rsqrt(square_total / total_channels + EPSILON)[:, None]
    mixed_out = (gated * inv_rms * gain_local).astype(jnp.bfloat16)
    projected = lax.psum_scatter(
        lax.dot_general(mixed_out, out_full, CONTRACT_LAST, preferred_element_type=jnp.float32),
        "tensor",
        scatter_dimension=0,
        tiled=True,
    )
    out_acts = (acts_row + projected).astype(jnp.bfloat16)[None]
    grad_row = grad_out[0]
    grad_rows_all = lax.all_gather(grad_row, "tensor", axis=0, tiled=True)
    grad_mixed = jnp.dot(grad_rows_all, out_full, preferred_element_type=jnp.float32).astype(
        jnp.bfloat16
    )
    grad_out_w = lax.dot_general(
        grad_rows_all, mixed_out, CONTRACT_FIRST, preferred_element_type=jnp.float32
    )
    grad_normed = grad_mixed.astype(jnp.float32)
    grad_gain_local = jnp.sum(grad_normed * gated * inv_rms, axis=0)
    scaled = grad_normed * gain_local
    row_dot = lax.psum(jnp.sum(scaled * gated, axis=1), "tensor")
    grad_gated = (
        inv_rms * scaled
        - gated * (inv_rms * inv_rms * inv_rms) * (row_dot / total_channels)[:, None]
    )
    (
        grad_x_low,
        grad_b,
        grad_c,
        grad_dt_in,
        grad_dt_shift,
        grad_log_rate,
        grad_skip,
        grad_gate_in,
    ) = mix_back(grad_gated)
    grad_x_in, grad_bc_part, grad_x_taps, grad_x_shift, grad_bc_taps, grad_bc_shift = conv_back(
        (grad_x_low, jnp.concatenate([grad_b, grad_c], axis=1))
    )
    grad_bc_in = lax.psum(grad_bc_part, "tensor").astype(jnp.bfloat16)
    grad_zx = jnp.stack([grad_gate_in.astype(jnp.bfloat16), grad_x_in.astype(jnp.bfloat16)], axis=1)
    grad_dt_low = grad_dt_in.astype(jnp.bfloat16)
    grad_zx_w = jnp.einsum("ld,lkc->dkc", hidden, grad_zx, preferred_element_type=jnp.float32)
    grad_bc_w = lax.dot_general(
        hidden, grad_bc_in, CONTRACT_FIRST, preferred_element_type=jnp.float32
    )
    grad_dt_w = lax.dot_general(
        hidden, grad_dt_low, CONTRACT_FIRST, preferred_element_type=jnp.float32
    )
    from_zx = jnp.einsum("lkc,dkc->ld", grad_zx, zx_full, preferred_element_type=jnp.float32)
    grad_hidden = lax.psum_scatter(
        from_zx
        + lax.dot_general(grad_dt_low, dt_full, CONTRACT_LAST, preferred_element_type=jnp.float32),
        "tensor",
        scatter_dimension=0,
        tiled=True,
    )
    bc_piece = lax.dynamic_slice_in_dim(grad_bc_in, rank * local_rows, local_rows, 0)
    grad_hidden = grad_hidden + lax.dot_general(
        bc_piece, bc_full, CONTRACT_LAST, preferred_element_type=jnp.float32
    )
    grad_acts_norm, grad_norm_gain = pre_back(grad_hidden)
    grad_acts = (grad_row.astype(jnp.float32) + grad_acts_norm)[None]
    grad_w_zx, grad_w_bc, grad_w_dt, grad_w_out = (
        lax.psum_scatter(grad_zx_w, "dp", scatter_dimension=0, tiled=True),
        lax.psum_scatter(grad_bc_w, "dp", scatter_dimension=0, tiled=True),
        lax.psum_scatter(grad_dt_w, "dp", scatter_dimension=0, tiled=True),
        lax.psum_scatter(grad_out_w, "dp", scatter_dimension=0, tiled=True),
    )
    small_sums = lax.psum(
        (
            grad_norm_gain,
            widen(grad_x_taps, chan_start, total_channels),
            widen(grad_x_shift, chan_start, total_channels),
            grad_bc_taps,
            grad_bc_shift,
            widen(grad_dt_shift, head_start, total_heads),
            widen(grad_log_rate, head_start, total_heads),
            widen(grad_skip, head_start, total_heads),
            widen(grad_gain_local, chan_start, total_channels),
        ),
        ("dp", "tensor"),
    )
    grad_ng, grad_cx, grad_cxb, grad_cbc, grad_cbcb, grad_dtb, grad_alog, grad_dsk, grad_gg = (
        small_sums
    )
    return (
        out_acts,
        grad_acts,
        grad_ng,
        grad_w_zx,
        grad_w_bc,
        grad_w_dt,
        grad_w_out,
        grad_cx,
        grad_cxb,
        grad_cbc,
        grad_cbcb,
        grad_dtb,
        grad_alog,
        grad_dsk,
        grad_gg,
    )


def solution(mesh):
    in_specs = (
        P("dp", "tensor", None),
        P("dp", "tensor", None),
        P(),
        P("dp", None, "tensor"),
        P("dp", None),
        P("dp", "tensor"),
        P("dp", "tensor"),
        P(),
        P(),
        P(),
        P(),
        P(),
        P(),
        P(),
        P(),
    )
    out_specs = (
        P("dp", "tensor", None),
        P("dp", "tensor", None),
        P(),
        P("dp", None, "tensor"),
        P("dp", None),
        P("dp", "tensor"),
        P("dp", "tensor"),
        P(),
        P(),
        P(),
        P(),
        P(),
        P(),
        P(),
        P(),
    )
    return jax.shard_map(body, mesh=mesh, in_specs=in_specs, out_specs=out_specs, check_vma=False)
```

profile of v0, /device:TPU:0, one launch (start us, length us, event | category | flops | bytes accessed | tf_op | source)
XLA Modules:
  0.0 918.6 jit_solution(7278153467009917441)
XLA Ops:
  16.2 27.9 %all_gather.19 = bf16[1024,8]{0,1:T(8,128)(2,1)S(1)} all-gather(bf16[128,8]{0,1:T(8,128)(2,1)S(1)} %copy-done.49), channel_id=1, replica_groups=mesh['dp'=8,'tensor'=4] {'dp'}, dimensions={0}, use_global_device_ids=true | all-gather | bytes 18432 | tf_op jit(solution)/shard_map/all_gather | solution.py:125
  44.2 32.4 %all_gather.21 = bf16[1024,256]{1,0:T(8,128)(2,1)S(1)} all-gather(bf16[128,256]{1,0:T(8,128)(2,1)S(1)} %copy-done.20), channel_id=1, replica_groups=mesh['dp'=8,'tensor'=4] {'dp'}, dimensions={0}, use_global_device_ids=true | all-gather | bytes 589824 | tf_op jit(solution)/shard_map/all_gather | solution.py:124
  86.3 15.2 %all-gather.8.cloned.1.call-done = bf16[1024,2,512]{2,0,1:T(8,128)(2,1)} async-done(((bf16[128,2,512]{2,0,1:T(8,128)(2,1)}), bf16[1024,2,512]{2,0,1:T(8,128)(2,1)}) %all-gather.8.cloned.1.call-update) | async-done | bytes 2097168 | tf_op jit(solution)/shard_map/all_gather | solution.py:123
  117.0 7.1 reshape.372
  137.4 87.5 %while.43 = (s32[]{:T(128)}, f32[8,64,128]{2,1,0:T(8,128)S(1)}, f32[8,256,8,64]{1,3,2,0:T(8,128)}, f32[8,8,64,128]{3,2,1,0:T(8,128)}, f32[8,256,8]{1,2,0:T(8,128...) while((s32[]{:T(128)}, f32[8,64,128]{2,1,0:T(8,128)S(1)}, ...), condition=%wide.region_4.5_spmd.clone.clone, body=%wide.region_1.4_spmd.clone.clone.sunk | while | flops 909711360 | bytes 5641051 | solution.py:58
  231.9 7.5 reshape.369
  239.4 7.6 multiply_reduce_fusion.8
  252.7 7.2 fusion.130
  260.0 7.4 fusion.96
  274.3 11.7 %multiply_reduce_fusion.3 = (f32[512]{0:T(512)}, f32[2048,512]{1,0:T(8,128)}, bf16[2048,1,512]{2,0,1:T(8,128)(2,1)}) fusion(f32[2048,512]{1,0:T(8,128)} %get-tuple-element.766, f32[2048,2,512]{2,0,1:T(8,128)} %copy-done.1, f32[2048]{0:T(1024)S(1)} %broadcast_multiply_fusion.8, f32[2048,512]{1,0:T(8,128)} %get-tuple-element.762, ...), kind=kLoop, calls=%fused_computation.161 | loop fusion | flops 30408192 | bytes 25196544 | tf_op jit(solution)/shard_map/transpose(jvp())/reduce_sum | solution.py:85
  286.0 7.1 reshape.370
  305.2 198.0 %while.42 = (s32[]{:T(128)}, f32[8]{0:T(128)}, f32[8,64,128]{2,1,0:T(8,128)S(1)}, f32[8,256,8,64]{1,3,2,0:T(8,128)}, f32[8,256,8]{1,2,0:T(8,128)}, /*index=5*/f3...) while((s32[]{:T(128)}, f32[8]{0:T(128)}, ...), condition=%wide.region_24.25_spmd.clone, body=%wide.region_10.0_spmd.clone.sunk | while | flops 2126610432 | bytes 15952340 | solution.py:58
  510.1 7.5 reshape.371
  517.7 11.5 %multiply_reduce_fusion.6 = (f32[512]{0:T(512)S(1)}, f32[512]{0:T(512)S(1)}, f32[512]{0:T(512)S(1)}, f32[512]{0:T(512)S(1)}, f32[512]{0:T(512)S(1)}, /*index=5*/f32[2048,512]{1,0:T(8,128)S(1)}) fusion(f32[2048,512]{1,0:T(8,128)} %copy-done, f32[2048,2,512]{2,0,1:T(8,128)} %copy-done.1, f32[2048,512]{1,0:T(8,128)} %get-tuple-element.766, ...), kind=kLoop, calls=%fused_computation.164 | loop fusion | flops 20968960 | bytes 25178112 | tf_op jit(solution)/shard_map/transpose(jvp())/reduce_sum | solution.py:21
  535.0 7.1 fusion.127
  542.2 8.2 fusion.107
  562.4 7.8 fusion.148
  579.6 40.8 %all-reduce.21 = bf16[2048,256]{1,0:T(8,128)(2,1)S(1)} all-reduce(f32[2048,256]{1,0:T(8,128)S(1)} %pad_add_fusion.3), channel_id=1, replica_groups=mesh['dp'=8,'tensor'=4] {'tensor'}, use_global_device_ids=true, to_apply=%region_26.27 | all-reduce | flops 524288 | bytes 3145728 | tf_op jit(solution)/shard_map/psum | solution.py:197
  628.7 8.8 reduce-scatter.11.cloned.1.call-done
  639.7 71.4 %reduce-scatter.9.cloned.1.call-done = f32[512,1024]{1,0:T(8,128)} async-done(((f32[2048,1024]{1,0:T(8,128)}), f32[512,1024]{1,0:T(8,128)}) %reduce-scatter.9.cloned.1.call-update) | async-done | bytes 2097168 | tf_op jit(solution)/shard_map/reduce_scatter | solution.py:208
  713.8 41.1 %all-reduce.19 = (f32[1024]{0:T(1024)}, f32[4,2048]{1,0:T(4,128)}, f32[2048]{0:T(1024)}, f32[4,256]{1,0:T(4,128)}, f32[256]{0:T(256)}, /*index=5*/f32[32]{0:T(128)}, f32[32]{0:T(128)}, f32[32]{0:T(128)}, f32[2048]{0:T(1024)}) all-reduce(f32[1024]{0:T(1024)S(1)} %get-tuple-element.689, ...), channel_id=1, replica_groups=mesh['dp'=8,'tensor'=4] {'dp','tensor'}, use_global_device_ids=true, to_apply=%region_29.30 | all-reduce | flops 14688 | bytes 117504 | tf_op jit(solution)/shard_map/psum | solution.py:227
  754.9 30.9 %reduce-scatter.7.cloned.1.call-done = f32[512,1024]{1,0:T(8,128)} async-done(((f32[2048,1024]{1,0:T(8,128)}), f32[512,1024]{1,0:T(8,128)}) %reduce-scatter.7.cloned.1.call-update) | async-done | bytes 2097168 | tf_op jit(solution)/shard_map/reduce_scatter | solution.py:161
  790.0 54.2 %reduce-scatter.15.cloned.1.call-done = f32[128,8]{0,1:T(8,128)} async-done(((f32[1024,8]{0,1:T(8,128)}), f32[128,8]{0,1:T(8,128)}) %reduce-scatter.15.cloned.1.call-update) | async-done | bytes 4112 | tf_op jit(solution)/shard_map/reduce_scatter | solution.py:224
  844.3 67.1 %reduce-scatter.13.cloned.1.call-done = f32[128,256]{1,0:T(8,128)} async-done(((f32[1024,256]{1,0:T(8,128)}), f32[128,256]{1,0:T(8,128)}) %reduce-scatter.13.cloned.1.call-update) | async-done | bytes 131088 | tf_op jit(solution)/shard_map/reduce_scatter | solution.py:223
  (623 shorter events, 414.4 us)
Async XLA Ops:
  7.2 36.9 %copy-start.20 = (bf16[128,256]{1,0:T(8,128)(2,1)S(1)}, bf16[128,256]{1,0:T(8,128)(2,1)}, u32[]{:S(2)}) copy-start(bf16[128,256]{1,0:T(8,128)(2,1)} %param.23) | copy-start | bytes 196612
  7.3 70.3 %all-gather.6.cloned.1.call-start = ((), (), s32[]{:S(2)}) async-start(), calls=%async_computation.6 | async-start | bytes 5242880 | tf_op jit(solution)/shard_map/all_gather | solution.py:130
  11.4 90.1 %all-gather.8.cloned.1.call-start = ((), (), s32[]{:S(2)}) async-start(), calls=%async_computation.7 | async-start | bytes 2359296 | tf_op jit(solution)/shard_map/all_gather | solution.py:123
  12.2 240.5 %all-gather.12.cloned.1.call-start = ((), (), s32[]{:S(2)}) async-start(), calls=%async_computation.15 | async-start | bytes 5242880 | tf_op jit(solution)/shard_map/all_gather | solution.py:169
  13.0 247.0 %all-gather.10.cloned.1.call-start = ((), (), s32[]{:S(2)}) async-start(), calls=%async_computation.8 | async-start | bytes 1179648 | tf_op jit(solution)/shard_map/all_gather | solution.py:126
  13.6 613.3 %reduce-scatter.17.cloned.1.call-start = ((), (), s32[]{:S(2)}) async-start(), calls=%async_computation.14 | async-start | bytes 2359296 | tf_op jit(solution)/shard_map/reduce_scatter | solution.py:225
  15.2 259.0 %copy-start.26 = (f32[512]{0:T(512)}, f32[512]{0:T(512)S(1)}, u32[]{:S(2)}) copy-start(f32[512]{0:T(512)S(1)} %dynamic_slice.100) | copy-start | bytes 6148
  16.1 258.1 %copy-start.22 = (f32[512]{0:T(512)}, f32[512]{0:T(512)S(1)}, u32[]{:S(2)}) copy-start(f32[512]{0:T(512)S(1)} %mul.863) | copy-start | bytes 6148
  16.2 65.2 %copy-start.39 = (f32[1,256]{1,0:T(1,128)}, f32[1,256]{1,0:T(1,128)S(1)}, u32[]{:S(2)}) copy-start(f32[1,256]{1,0:T(1,128)S(1)} %get-tuple-element.793) | copy-start | bytes 3076
  16.2 65.2 %copy-start.41 = (f32[1,256]{1,0:T(1,128)}, f32[1,256]{1,0:T(1,128)S(1)}, u32[]{:S(2)}) copy-start(f32[1,256]{1,0:T(1,128)S(1)} %get-tuple-element.794) | copy-start | bytes 3076
  16.2 65.2 %copy-start.43 = (f32[1,256]{1,0:T(1,128)}, f32[1,256]{1,0:T(1,128)S(1)}, u32[]{:S(2)}) copy-start(f32[1,256]{1,0:T(1,128)S(1)} %get-tuple-element.795) | copy-start | bytes 3076
  16.2 65.2 %copy-start.45 = (f32[1,256]{1,0:T(1,128)}, f32[1,256]{1,0:T(1,128)S(1)}, u32[]{:S(2)}) copy-start(f32[1,256]{1,0:T(1,128)S(1)} %get-tuple-element.796) | copy-start | bytes 3076
  44.1 86.8 %copy-start.18 = (bf16[1024,8]{0,1:T(8,128)(2,1)}, bf16[1024,8]{0,1:T(8,128)(2,1)S(1)}, u32[]{:S(2)}) copy-start(bf16[1024,8]{0,1:T(8,128)(2,1)S(1)} %all_gather.19) | copy-start | bytes 49156
  44.2 37.3 %copy-start.51 = (f32[256]{0:T(256)S(1)}, f32[256]{0:T(256)}, u32[]{:S(2)}) copy-start(f32[256]{0:T(256)} %param.29) | copy-start | bytes 3076
  77.5 34.7 %copy-start.28 = (f32[1,512]{1,0:T(1,128)}, f32[1,512]{1,0:T(1,128)S(1)}, u32[]{:S(2)}) copy-start(f32[1,512]{1,0:T(1,128)S(1)} %get-tuple-element.787) | copy-start | bytes 6148
  260.0 377.4 %reduce-scatter.11.cloned.1.call-start = ((), (), s32[]{:S(2)}) async-start(), calls=%async_computation.11 | async-start | bytes 4718592 | tf_op jit(solution)/shard_map/reduce_scatter | solution.py:222
  550.4 160.6 %reduce-scatter.9.cloned.1.call-start = ((), (), s32[]{:S(2)}) async-start(), calls=%async_computation.10 | async-start | bytes 10485760 | tf_op jit(solution)/shard_map/reduce_scatter | solution.py:208
  561.2 224.6 %reduce-scatter.7.cloned.1.call-start = ((), (), s32[]{:S(2)}) async-start(), calls=%async_computation.9 | async-start | bytes 10485760 | tf_op jit(solution)/shard_map/reduce_scatter | solution.py:161
  570.2 274.0 %reduce-scatter.15.cloned.1.call-start = ((), (), s32[]{:S(2)}) async-start(), calls=%async_computation.13 | async-start | bytes 36864 | tf_op jit(solution)/shard_map/reduce_scatter | solution.py:224
  620.4 90.6 %copy-start.4 = (bf16[1,512,1024]{2,1,0:T(8,128)(2,1)S(1)}, bf16[1,512,1024]{2,1,0:T(8,128)(2,1)}, u32[]{:S(2)}) copy-start(bf16[1,512,1024]{2,1,0:T(8,128)(2,1)} %param.19) | copy-start | bytes 3145732
  620.5 90.6 %copy-start.21 = (f32[1024]{0:T(1024)S(1)}, f32[1024]{0:T(1024)}, u32[]{:S(2)}) copy-start(f32[1024]{0:T(1024)} %param.21) | copy-start | bytes 12292
  620.5 90.6 %copy-start.25 = (f32[512]{0:T(512)S(1)}, f32[512]{0:T(512)}, u32[]{:S(2)}) copy-start(f32[512]{0:T(512)} %copy-done.24) | copy-start | bytes 6148
  620.5 290.9 %reduce-scatter.13.cloned.1.call-start = ((), (), s32[]{:S(2)}) async-start(), calls=%async_computation.12 | async-start | bytes 1179648 | tf_op jit(solution)/shard_map/reduce_scatter | solution.py:223
  625.4 129.5 %copy-start.37 = (f32[512]{0:T(512)S(1)}, f32[512]{0:T(512)}, u32[]{:S(2)}) copy-start(f32[512]{0:T(512)} %copy-done.36) | copy-start | bytes 6148
  (43 other events, 320.7 us)
Sparse Core Ops, SparseCore 0:
  11.6 37.1 all-gather.5
  51.5 49.9 all-gather.7
  103.1 32.9 all-gather.11
  138.1 40.3 all-gather.9
  260.1 68.2 reduce-scatter.16
  550.6 86.8 reduce-scatter.10
  640.0 71.0 reduce-scatter.8
  713.6 72.0 reduce-scatter.6
  789.5 54.7 reduce-scatter.14
  848.1 63.1 reduce-scatter.12
where the time goes:
time: 926 us; the launch traced here: 919 us
  waiting for transfers between devices  249 us (27%)
  matrix products  235 us (25%)
  blocking collectives  155 us (17%)
  other arithmetic  140 us (15%)
  local copies, waits for them, and re-layouts  123 us (13%)
  between operations  15.3 us (2%)
    dot_general x24, matrix products, step_block(): jnp.einsum('ijh,jhp->ihp', weights, x_block, precision=FULL_PRECISION)  78.3 us
    reduce_scatter x1, waiting for transfers between devices, body(): lax.psum_scatter(from_zx + lax.dot_general(grad_dt_low, dt_full, CONTRACT...  71.4 us
    reduce_scatter x1, waiting for transfers between devices, body(): lax.psum_scatter(grad_bc_w, 'dp', scatter_dimension=0, tiled=True)  67.1 us
    reduce_scatter x1, waiting for transfers between devices, body(): lax.psum_scatter(grad_dt_w, 'dp', scatter_dimension=0, tiled=True)  54.2 us
    psum x1, blocking collectives, body(): lax.psum((grad_norm_gain, widen(grad_x_taps, chan_start, total_channels),...  41.1 us
    psum x1, blocking collectives, body(): grad_bc_in = lax.psum(grad_bc_part, 'tensor').astype(jnp.bfloat16)  40.8 us
    another operation x73, other arithmetic  39.1 us
    dot_general x32, matrix products, step_block(): jnp.einsum('in,hpn->ihp', c_block, state, precision=FULL_PRECISION)  35.8 us
  transfers between devices with their start and end apart: 10, of which 6 were waited for; matrix products, arithmetic and copies ran while one was open for 53% of the time, Pallas kernels for 0%

commit v1 on v0

v1 whole, which is shorter than its diff:
```python
import functools

import jax
import jax.numpy as jnp
from jax import lax
from jax.experimental import pallas as pl
from jax.experimental.pallas import tpu as pltpu
from jax.sharding import PartitionSpec as P

EPSILON = 1e-05
F32, BF16 = jnp.float32, jnp.bfloat16
CHUNK = 128
STEP = 256
LANES = 128
FAR = -1e30
NN = (((1,), (0,)), ((), ()))
NT = (((1,), (1,)), ((), ()))
TN = (((0,), (0,)), ((), ()))


def mm(a, b, dims=NN):
    return lax.dot_general(a, b, dims, preferred_element_type=F32)


def mm_full(a, b, dims=NN):
    return lax.dot_general(
        a, b, dims, preferred_element_type=F32, precision=lax.Precision.HIGHEST
    )


def sigmoid(v):
    return 1.0 / (1.0 + jnp.exp(-v))


def softplus(v):
    u = jnp.exp(-jnp.abs(v))
    small = u * (1.0 - u * (0.5 - u * (1.0 / 3.0)))
    return jnp.maximum(v, 0.0) + jnp.where(u < 1e-2, small, jnp.log(1.0 + u))


def iota(shape, dim):
    return lax.broadcasted_iota(jnp.int32, shape, dim)


def spread(table, pair, half):
    return jnp.where(half, table[:, 2 * pair : 2 * pair + 1], table[:, 2 * pair + 1 : 2 * pair + 2])


def fold_rows(v):
    rows, cols = v.shape
    return jnp.sum(v.reshape(rows // 8, 8, cols), axis=0)


def chunk_rates(dt_in, dt_bias, rate):
    step = softplus(dt_in + dt_bias)
    log_step = step * rate
    lower = (iota((CHUNK, CHUNK), 0) >= iota((CHUNK, CHUNK), 1)).astype(F32)
    cum = mm_full(lower, log_step)
    return step, log_step, cum


def fwd_kernel(
    heads, channels, states,
    hid_ref, w_ref, grad_ref, wout_ref, conv_ref, row_ref, chan_ref,
    proj_ref, pre_ref, mixed_ref, gm_ref, stat_ref, start_ref,
    shift, state,
):
    conv_cols = channels + 2 * states

    @pl.when(pl.program_id(0) == 0)
    def _():
        shift[0:8, :] = jnp.zeros((8, conv_cols), F32)
        state[...] = jnp.zeros_like(state)

    proj = mm(hid_ref[...], w_ref[...])
    proj_ref[...] = proj
    gm_ref[...] = mm(grad_ref[...], wout_ref[...]).astype(BF16)
    conv_in = proj[:, channels : channels + conv_cols]
    shift[8 : 8 + STEP, :] = conv_in
    pre = conv_ref[4:5, :] + conv_ref[3:4, :] * conv_in
    for back in range(1, 4):
        pre = pre + conv_ref[3 - back : 4 - back, :] * shift[8 - back : 8 - back + STEP, :]
    shift[0:8, :] = conv_in[STEP - 8 :, :]
    pre_ref[...] = pre
    half = iota((CHUNK, LANES), 1) < LANES // 2
    lower = iota((CHUNK, CHUNK), 0) >= iota((CHUNK, CHUNK), 1)
    lane = iota((CHUNK, LANES), 1)
    for sub in range(STEP // CHUNK):
        rows = pl.ds(sub * CHUNK, CHUNK)
        pre_c = pre_ref[rows, :]
        act = (pre_c * sigmoid(pre_c)).astype(BF16)
        x_low = act[:, :channels]
        b_mat = act[:, channels : channels + states]
        c_mat = act[:, channels + states :]
        dt_in = proj_ref[rows, channels + conv_cols :]
        step, log_step, cum = chunk_rates(dt_in, row_ref[0:1, :], row_ref[1:2, :])
        cum_t = cum.T
        step_t = step.T
        last = cum[CHUNK - 1 : CHUNK, :]
        grow = jnp.exp(cum)
        tail = jnp.exp(last - cum) * step
        total = jnp.exp(last)
        scores = mm(c_mat, b_mat, NT)
        state_low = state[...].astype(BF16)
        start_ref[sub] = state_low
        from_state = mm(c_mat, state_low, NT)
        square = jnp.zeros((CHUNK, 1), F32)
        dots = jnp.zeros((CHUNK, 1), F32)
        for pair in range(heads // 2):
            cols = slice(pair * LANES, (pair + 1) * LANES)
            x_pair = x_low[:, cols]
            zero = jnp.zeros_like(x_pair)
            parts = []
            for side in range(2):
                head = 2 * pair + side
                gap = jnp.where(lower, cum[:, head : head + 1] - cum_t[head : head + 1, :], FAR)
                parts.append((scores * jnp.exp(gap) * step_t[head : head + 1, :]).astype(BF16))
            x_wide = x_pair.astype(F32)
            both = jnp.concatenate(parts, axis=1)
            x_two = jnp.concatenate(
                [jnp.where(half, x_wide, 0.0).astype(BF16), jnp.where(half, 0.0, x_wide).astype(BF16)],
                axis=0,
            )
            mixed = (
                mm(both, x_two)
                + from_state[:, cols] * spread(grow, pair, half)
                + chan_ref[0:1, cols] * x_wide
            )
            mixed_ref[rows, cols] = mixed
            gate = proj_ref[rows, cols]
            gated = mixed * (gate * sigmoid(gate))
            square = square + jnp.sum(gated * gated, axis=1, keepdims=True)
            gm = gm_ref[rows, cols].astype(F32)
            dots = dots + jnp.sum(gm * chan_ref[1:2, cols] * gated, axis=1, keepdims=True)
            weighted = (x_wide * spread(tail, pair, half)).astype(BF16)
            update = mm(weighted, b_mat, TN)
            for side in range(2):
                head = 2 * pair + side
                place = pl.ds(pair * LANES + side * 64, 64)
                state[place, :] = (
                    state[place, :] * total[:, head : head + 1] + update[side * 64 : side * 64 + 64, :]
                )
        stat = jnp.where(lane == 0, square, jnp.where(lane == 1, dots, 0.0))
        stat_ref[:, sub * CHUNK : (sub + 1) * CHUNK] = stat.T[0:8, :]


def bwd_kernel(
    heads, channels, states, total_channels,
    proj_ref, pre_ref, mixed_ref, gm_ref, stat_ref, start_ref, conv_ref, row_ref, chan_ref,
    mix_out_ref, grad_ref, acc_conv_ref, acc_chan_ref, acc_row_ref,
    later, grad_state,
):
    conv_cols = channels + 2 * states
    dt_at = channels + conv_cols

    @pl.when(pl.program_id(0) == 0)
    def _():
        later[CHUNK : CHUNK + 8, :] = jnp.zeros((8, conv_cols), F32)
        grad_state[...] = jnp.zeros_like(grad_state)
        acc_conv_ref[...] = jnp.zeros_like(acc_conv_ref)
        acc_chan_ref[...] = jnp.zeros_like(acc_chan_ref)
        acc_row_ref[...] = jnp.zeros_like(acc_row_ref)

    half = iota((CHUNK, LANES), 1) < LANES // 2
    upper = iota((CHUNK, CHUNK), 1) >= iota((CHUNK, CHUNK), 0)
    upper_ones = upper.astype(F32)
    lane = iota((CHUNK, LANES), 1)
    chan_head = iota((LANES, LANES), 0) // 64
    for sub in reversed(range(STEP // CHUNK)):
        rows = pl.ds(sub * CHUNK, CHUNK)
        pre_c = pre_ref[rows, :]
        sig_pre = sigmoid(pre_c)
        act_wide = pre_c * sig_pre
        slope = sig_pre * (1.0 + pre_c * (1.0 - sig_pre))
        act = act_wide.astype(BF16)
        b_mat = act[:, channels : channels + states]
        c_mat = act[:, channels + states :]
        dt_raw = proj_ref[rows, dt_at:] + row_ref[0:1, :]
        step, log_step, cum = chunk_rates(proj_ref[rows, dt_at:], row_ref[0:1, :], row_ref[1:2, :])
        cum_t = cum.T
        last = cum[CHUNK - 1 : CHUNK, :]
        grow = jnp.exp(cum)
        fade = jnp.exp(last - cum)
        tail = fade * step
        total = jnp.exp(last)
        stat = jnp.concatenate(
            [stat_ref[:, sub * CHUNK : (sub + 1) * CHUNK], jnp.zeros((CHUNK - 8, CHUNK), F32)], axis=0
        ).T
        inv = lax.rsqrt(stat[:, 0:1] / total_channels + EPSILON)
        pull = inv * inv * inv * (stat[:, 1:2] / total_channels)
        state_low = start_ref[sub]
        grad_low = grad_state[...].astype(BF16)
        scores_t = mm(b_mat, c_mat, NT)
        from_state = mm(c_mat, state_low, NT)
        from_grad = mm(b_mat, grad_low, NT)
        grad_scores = jnp.zeros((CHUNK, CHUNK), F32)
        plain_sum = jnp.zeros((CHUNK, LANES), F32)
        in_sum = jnp.zeros((CHUNK, LANES), F32)
        out_sum = jnp.zeros((CHUNK, LANES), F32)
        row_parts = []
        const_row = jnp.zeros((1, LANES), F32)
        lane_row = iota((1, LANES), 1)
        grad_c = jnp.zeros((CHUNK, states), F32)
        grad_b = jnp.zeros((CHUNK, states), F32)
        for pair in range(heads // 2):
            cols = slice(pair * LANES, (pair + 1) * LANES)
            gate = proj_ref[rows, cols]
            mixed = mixed_ref[rows, cols]
            gm = gm_ref[rows, cols].astype(F32)
            gain = chan_ref[1:2, cols]
            sig_gate = sigmoid(gate)
            silu_gate = gate * sig_gate
            gated = mixed * silu_gate
            normed = gated * inv
            mix_out_ref[rows, cols] = (normed * gain).astype(BF16)
            acc_chan_ref[0, :, cols] += fold_rows(gm * normed)
            grad_gated = inv * (gm * gain) - gated * pull
            grad_ref[rows, cols] = (
                grad_gated * mixed * (sig_gate * (1.0 + gate * (1.0 - sig_gate)))
            ).astype(BF16)
            gh = grad_gated * silu_gate
            x_pair = act[:, cols]
            x_wide = x_pair.astype(F32)
            acc_chan_ref[1, :, cols] += fold_rows(gh * x_wide)
            gh_low = gh.astype(BF16)
            parts = []
            for side in range(2):
                head = 2 * pair + side
                keep = half if side == 0 else jnp.logical_not(half)
                x_side = jnp.where(keep, x_wide, 0.0).astype(BF16)
                cross = mm(x_side, gh_low, NT)
                gap = jnp.where(upper, cum_t[head : head + 1, :] - cum[:, head : head + 1], FAR)
                decay = jnp.exp(gap)
                parts.append((scores_t * decay).astype(BF16))
                bare = decay * cross
                timed = bare * step[:, head : head + 1]
                grad_scores = grad_scores + timed
                plain_sum = jnp.where(
                    lane == head, jnp.sum(bare * scores_t, axis=1, keepdims=True), plain_sum
                )
                row_parts.append(jnp.sum(timed * scores_t, axis=0, keepdims=True))
            g_two = jnp.concatenate(
                [jnp.where(half, gh, 0.0).astype(BF16), jnp.where(half, 0.0, gh).astype(BF16)], axis=0
            )
            within = mm(jnp.concatenate(parts, axis=1), g_two)
            state_pair = state_low[cols, :]
            grad_pair = grad_low[cols, :]
            fg = from_grad[:, cols]
            grad_x = (
                spread(step, pair, half) * (within + spread(fade, pair, half) * fg)
                + chan_ref[0:1, cols] * gh
            )
            later[0:CHUNK, cols] = grad_x * slope[:, cols]
            pick = (chan_head + 2 * pair == iota((LANES, LANES), 1)).astype(BF16)
            both = jnp.concatenate([x_wide * fg, gh * from_state[:, cols]], axis=0)
            high = both.astype(BF16)
            sums = mm(high, pick) + mm((both - high.astype(F32)).astype(BF16), pick)
            in_sum = in_sum + sums[:CHUNK]
            out_sum = out_sum + sums[CHUNK:]
            grown = (gh * spread(grow, pair, half)).astype(BF16)
            weighted = (x_wide * spread(tail, pair, half)).astype(BF16)
            grad_c = grad_c + mm(grown, state_pair)
            grad_b = grad_b + mm(weighted, grad_pair)
            update = mm(grown, c_mat, TN)
            for side in range(2):
                head = 2 * pair + side
                place = pl.ds(pair * LANES + side * 64, 64)
                held = grad_state[place, :]
                old = state_low[pair * LANES + side * 64 : pair * LANES + side * 64 + 64, :]
                meet = jnp.sum(jnp.sum(held * old.astype(F32), axis=0, keepdims=True), axis=1, keepdims=True)
                const_row = jnp.where(lane_row == head, meet, const_row)
                grad_state[place, :] = (
                    held * total[:, head : head + 1] + update[side * 64 : side * 64 + 64, :]
                )
        scores_low = grad_scores.astype(BF16)
        grad_b = grad_b + mm(scores_low, c_mat)
        grad_c = grad_c + mm(scores_low, b_mat, TN)
        later[0:CHUNK, channels : channels + states] = grad_b * slope[:, channels : channels + states]
        later[0:CHUNK, channels + states :] = grad_c * slope[:, channels + states :]
        row_sum = jnp.concatenate(row_parts + [jnp.zeros((CHUNK - heads, CHUNK), F32)], axis=0).T
        plain_in = in_sum * fade
        timed_in = plain_in * step
        flow = row_sum - plain_sum * step + out_sum * grow - timed_in
        grad_log = (
            mm_full(upper_ones, flow)
            + jnp.sum(timed_in, axis=0, keepdims=True)
            + const_row * total
        )
        grad_step = plain_sum + plain_in + row_ref[1:2, :] * grad_log
        grad_dt = grad_step * sigmoid(dt_raw)
        grad_ref[rows, dt_at:] = grad_dt.astype(BF16)
        acc_row_ref[0] += fold_rows(grad_dt)
        acc_row_ref[1] += fold_rows(grad_log * log_step)
        conv_in = proj_ref[rows, channels:dt_at]
        grad_pre = later[0:CHUNK, :]
        grad_in = conv_ref[3:4, :] * grad_pre
        acc_conv_ref[3] += fold_rows(conv_in * grad_pre)
        acc_conv_ref[4] += fold_rows(grad_pre)
        for ahead in range(1, 4):
            moved = later[ahead : ahead + CHUNK, :]
            grad_in = grad_in + conv_ref[3 - ahead : 4 - ahead, :] * moved
            acc_conv_ref[3 - ahead] += fold_rows(conv_in * moved)
        grad_ref[rows, channels:dt_at] = grad_in.astype(BF16)
        later[CHUNK : CHUNK + 8, :] = later[0:8, :]


def whole(shape):
    return pl.BlockSpec(shape, lambda i: (0,) * len(shape))


def run_forward(hidden, weights, grad_rows, w_out, conv_rows, head_rows, chan_rows, heads, channels, states):
    length, width = hidden.shape
    cols = weights.shape[1]
    conv_cols = channels + 2 * states
    steps = length // STEP
    subs = STEP // CHUNK

    def by_rows(n):
        return pl.BlockSpec((STEP, n), lambda i: (i, 0))

    return pl.pallas_call(
        functools.partial(fwd_kernel, heads, channels, states),
        grid=(steps,),
        in_specs=[
            by_rows(width), whole(weights.shape), by_rows(width), whole(w_out.shape),
            whole(conv_rows.shape), whole(head_rows.shape), whole(chan_rows.shape),
        ],
        out_specs=[
            by_rows(cols), by_rows(conv_cols), by_rows(channels), by_rows(channels),
            pl.BlockSpec((8, STEP), lambda i: (0, i)),
            pl.BlockSpec((subs, channels, states), lambda i: (i, 0, 0)),
        ],
        out_shape=[
            jax.ShapeDtypeStruct((length, cols), F32),
            jax.ShapeDtypeStruct((length, conv_cols), F32),
            jax.ShapeDtypeStruct((length, channels), F32),
            jax.ShapeDtypeStruct((length, channels), BF16),
            jax.ShapeDtypeStruct((8, length), F32),
            jax.ShapeDtypeStruct((length // CHUNK, channels, states), BF16),
        ],
        scratch_shapes=[pltpu.VMEM((8 + STEP, conv_cols), F32), pltpu.VMEM((channels, states), F32)],
        compiler_params=pltpu.CompilerParams(dimension_semantics=("arbitrary",), vmem_limit_bytes=56 << 20),
        cost_estimate=pl.CostEstimate(
            flops=2 * length * width * (cols + channels) + length * heads * 60000,
            bytes_accessed=length * (width * 4 + cols * 4 + conv_cols * 4 + channels * 6),
            transcendentals=length * heads * 256,
        ),
        name="mixer_forward",
    )(hidden, weights, grad_rows, w_out, conv_rows, head_rows, chan_rows)


def run_backward(proj, pre, mixed, gm, stats, starts, conv_rows, head_rows, chan_rows, heads, channels, states, total_channels):
    length, cols = proj.shape
    conv_cols = channels + 2 * states
    steps = length // STEP
    subs = STEP // CHUNK

    def by_rows(n):
        return pl.BlockSpec((STEP, n), lambda i: (steps - 1 - i, 0))

    return pl.pallas_call(
        functools.partial(bwd_kernel, heads, channels, states, total_channels),
        grid=(steps,),
        in_specs=[
            by_rows(cols), by_rows(conv_cols), by_rows(channels), by_rows(channels),
            pl.BlockSpec((8, STEP), lambda i: (0, steps - 1 - i)),
            pl.BlockSpec((subs, channels, states), lambda i: (steps - 1 - i, 0, 0)),
            whole(conv_rows.shape), whole(head_rows.shape), whole(chan_rows.shape),
        ],
        out_specs=[
            by_rows(channels), by_rows(cols),
            whole((5, 8, conv_cols)), whole((2, 8, channels)), whole((2, 8, LANES)),
        ],
        out_shape=[
            jax.ShapeDtypeStruct((length, channels), BF16),
            jax.ShapeDtypeStruct((length, cols), BF16),
            jax.ShapeDtypeStruct((5, 8, conv_cols), F32),
            jax.ShapeDtypeStruct((2, 8, channels), F32),
            jax.ShapeDtypeStruct((2, 8, LANES), F32),
        ],
        scratch_shapes=[pltpu.VMEM((CHUNK + 8, conv_cols), F32), pltpu.VMEM((channels, states), F32)],
        compiler_params=pltpu.CompilerParams(dimension_semantics=("arbitrary",), vmem_limit_bytes=56 << 20),
        cost_estimate=pl.CostEstimate(
            flops=length * heads * 200000,
            bytes_accessed=length * (cols * 6 + conv_cols * 4 + channels * 8),
            transcendentals=length * heads * 256,
        ),
        name="mixer_backward",
    )(proj, pre, mixed, gm, stats, starts, conv_rows, head_rows, chan_rows)


def body(
    acts, grad_out, norm_gain, w_zx, w_bc, w_dt, w_out,
    conv_x, conv_x_bias, conv_bc, conv_bc_bias, dt_bias, a_log, d_skip, gate_gain,
):
    parts = lax.axis_size("tensor")
    rank = lax.axis_index("tensor")
    channels = w_zx.shape[2]
    heads = w_dt.shape[1]
    states = w_bc.shape[1] // 2
    head_width = channels // heads
    total_channels = channels * parts
    total_heads = heads * parts
    chan_start = rank * channels
    head_start = rank * heads
    shard = w_zx.shape[0]

    def mine(v, start, size):
        return lax.dynamic_slice_in_dim(v, start, size, v.ndim - 1)

    def pad_lanes(v):
        return jnp.pad(v, ((0, 0), (0, LANES - v.shape[1])))

    packed = jnp.concatenate([w_zx.reshape(shard, 2 * channels), w_bc, pad_lanes(w_dt)], axis=1)
    weights = lax.all_gather(packed, "dp", axis=0, tiled=True)
    out_full = lax.all_gather(w_out, "dp", axis=0, tiled=True)
    acts_row = acts[0].astype(F32)
    grad_row = grad_out[0]
    inv0 = lax.rsqrt(jnp.mean(acts_row * acts_row, axis=-1, keepdims=True) + EPSILON)
    hidden = lax.all_gather(
        (acts_row * inv0 * norm_gain).astype(BF16), "tensor", axis=0, tiled=True
    )
    grad_rows = lax.all_gather(grad_row, "tensor", axis=0, tiled=True)

    conv_rows = jnp.concatenate(
        [
            jnp.concatenate([mine(conv_x, chan_start, channels), conv_bc], axis=1),
            jnp.concatenate([mine(conv_x_bias, chan_start, channels), conv_bc_bias])[None],
            jnp.zeros((3, channels + 2 * states), F32),
        ],
        axis=0,
    )
    dt_bias_mine = mine(dt_bias, head_start, heads)
    rate_mine = -jnp.exp(mine(a_log, head_start, heads))
    head_rows = jnp.pad(jnp.stack([dt_bias_mine, rate_mine]), ((0, 6), (0, LANES - heads)))
    chan_rows = jnp.pad(
        jnp.stack(
            [jnp.repeat(mine(d_skip, head_start, heads), head_width), mine(gate_gain, chan_start, channels)]
        ),
        ((0, 6), (0, 0)),
    )
    proj, pre, mixed, gm, stats, starts = run_forward(
        hidden, weights, grad_rows, out_full, conv_rows, head_rows, chan_rows, heads, channels, states
    )
    stats = lax.psum(stats, "tensor")
    mixed_out, grads, acc_conv, acc_chan, acc_row = run_backward(
        proj, pre, mixed, gm, stats, starts, conv_rows, head_rows, chan_rows,
        heads, channels, states, total_channels,
    )
    projected = lax.psum_scatter(
        mm(mixed_out, out_full, NT).astype(BF16), "tensor", scatter_dimension=0, tiled=True
    )
    out_acts = (acts_row + projected.astype(F32)).astype(BF16)[None]
    grad_w_out = lax.psum_scatter(
        mm(grad_rows, mixed_out, TN).astype(BF16), "dp", scatter_dimension=0, tiled=True
    ).astype(F32)
    grad_hidden = lax.psum_scatter(
        mm(grads, weights, NT).astype(BF16), "tensor", scatter_dimension=0, tiled=True
    ).astype(F32)
    grad_weights = lax.psum_scatter(
        mm(hidden, grads, TN).astype(BF16), "dp", scatter_dimension=0, tiled=True
    ).astype(F32)
    grad_w_zx = grad_weights[:, : 2 * channels].reshape(shard, 2, channels)
    grad_w_dt = grad_weights[:, 2 * channels + 2 * states : 2 * channels + 2 * states + heads]
    grad_w_bc = lax.psum(grad_weights[:, 2 * channels : 2 * channels + 2 * states], "tensor")

    scaled = grad_hidden * norm_gain
    inner = jnp.sum(scaled * acts_row, axis=1, keepdims=True)
    grad_acts = (
        grad_row.astype(F32)
        + scaled * inv0
        - acts_row * (inv0 * inv0 * inv0 * (inner / acts_row.shape[1]))
    )[None]
    grad_ng = jnp.sum(grad_hidden * acts_row * inv0, axis=0)

    conv_sum = jnp.sum(acc_conv, axis=1)
    chan_sum = jnp.sum(acc_chan, axis=1)
    row_sum = jnp.sum(acc_row, axis=1)[:, :heads]
    skip_sum = jnp.sum(chan_sum[1].reshape(heads, head_width), axis=1)

    def widen(piece, start, size):
        holder = jnp.zeros(piece.shape[:-1] + (size,), F32)
        return lax.dynamic_update_slice_in_dim(holder, piece, start, piece.ndim - 1)

    wide = jnp.concatenate([conv_sum[:, :channels], chan_sum[0:1]], axis=0)
    head_sums = jnp.concatenate([row_sum, skip_sum[None]], axis=0)
    flat = jnp.concatenate(
        [
            grad_ng,
            widen(wide, chan_start, total_channels).reshape(-1),
            conv_sum[:, channels:].reshape(-1),
            widen(head_sums, head_start, total_heads).reshape(-1),
        ]
    )
    flat = lax.psum(flat, ("dp", "tensor"))
    at = 0
    pieces = []
    for shape in ((acts_row.shape[1],), (6, total_channels), (5, 2 * states), (3, total_heads)):
        size = 1
        for extent in shape:
            size *= extent
        pieces.append(flat[at : at + size].reshape(shape))
        at += size
    grad_ng, wide, conv_b, head_sums = pieces
    return (
        out_acts, grad_acts, grad_ng, grad_w_zx, grad_w_bc, grad_w_dt, grad_w_out,
        wide[:4], wide[4], conv_b[:4], conv_b[4],
        head_sums[0], head_sums[1], head_sums[2], wide[5],
    )


def solution(mesh):
    in_specs = (
        P("dp", "tensor", None), P("dp", "tensor", None), P(),
        P("dp", None, "tensor"), P("dp", None), P("dp", "tensor"), P("dp", "tensor"),
    ) + (P(),) * 8
    out_specs = (
        P("dp", "tensor", None), P("dp", "tensor", None), P(),
        P("dp", None, "tensor"), P("dp", None), P("dp", "tensor"), P("dp", "tensor"),
    ) + (P(),) * 8
    return jax.shard_map(body, mesh=mesh, in_specs=in_specs, out_specs=out_specs, check_vma=False)
```

time: 926 us -> 579 us (0.63)
  matrix products: 235 us -> 32.4 us
  waiting for transfers between devices: 249 us -> 379 us
  other arithmetic: 140 us -> 11.2 us
  blocking collectives: 155 us -> 40.5 us
  local copies, waits for them, and re-layouts: 123 us -> 18.4 us
  Pallas kernels: 0 us -> 82.2 us
    dot_general x124 -> x4, matrix products: 235 us -> 32.4 us  [mm(): return lax.dot_general(a, b, dims, preferred_element_type=F32)]
    all_gather x4, waiting for transfers between devices: 15.3 us -> 166 us  [the longest x1 58.8 us: body(): weights = lax.all_gather(packed, 'dp', axis=0, tiled=True)]
    reduce_scatter x6 -> x3, waiting for transfers between devices: 232 us -> 120 us  [the longest x1 72.9 us: body(): lax.psum_scatter(mm(hidden, grads, TN).astype(BF16), 'dp', scatter_dimens...]
    pallas_call x0 -> x2, Pallas kernels: none -> 82.2 us  [the longest x1 48.9 us: run_backward(): pl.pallas_call(functools.partial(bwd_kernel, heads, channels, states, tot...]
    all_gather x2 -> x0, blocking collectives: 60.4 us -> none  [the longest x1 32.4 us: body(): lax.all_gather(w_bc, 'dp', axis=0, tiled=True)]
    psum x0 -> x2, waiting for transfers between devices: none -> 60.2 us  [the longest x1 31.6 us: body(): stats = lax.psum(stats, 'tensor')]
    psum x4 -> x1, blocking collectives: 94.4 us -> 40.5 us  [body(): flat = lax.psum(flat, ('dp', 'tensor'))]
    reshape x14 -> x4, local copies, waits for them, and re-layouts: 48.9 us -> 1.33 us  [the longest x1 1.23 us: body(): grad_w_zx = grad_weights[:, :2 * channels].reshape(shard, 2, channels)]
  transfers between devices with their start and end apart: 10 -> 10, of which waited for: 6 -> 10; matrix products, arithmetic and copies ran while one was open for 53% -> 9% of each run, Pallas kernels for 0% -> 0%
where the time goes in v1:
time: 579 us
  waiting for transfers between devices  379 us (65%)
  Pallas kernels  82.2 us (14%)
  blocking collectives  40.5 us (7%)
  matrix products  32.4 us (6%)
  local copies, waits for them, and re-layouts  18.4 us (3%)
  between operations  14.4 us (2%)
  other arithmetic  11.2 us (2%)
    reduce_scatter x1, waiting for transfers between devices, body(): lax.psum_scatter(mm(hidden, grads, TN).astype(BF16), 'dp', scatter_dimens...  72.9 us
    all_gather x1, waiting for transfers between devices, body(): weights = lax.all_gather(packed, 'dp', axis=0, tiled=True)  58.8 us
    pallas_call x1, Pallas kernels, run_backward(): pl.pallas_call(functools.partial(bwd_kernel, heads, channels, states, tot...  48.9 us
    reduce_scatter x1, waiting for transfers between devices, body(): lax.psum_scatter(mm(grads, weights, NT).astype(BF16), 'tensor', scatter_d...  42.7 us
    psum x1, blocking collectives, body(): flat = lax.psum(flat, ('dp', 'tensor'))  40.5 us
    all_gather x1, waiting for transfers between devices, body(): grad_rows = lax.all_gather(grad_row, 'tensor', axis=0, tiled=True)  35.9 us
    all_gather x1, waiting for transfers between devices, body(): out_full = lax.all_gather(w_out, 'dp', axis=0, tiled=True)  35.6 us
    all_gather x1, waiting for transfers between devices, body(): lax.all_gather((acts_row * inv0 * norm_gain).astype(BF16), 'tensor', axis...  35.2 us
  transfers between devices with their start and end apart: 10, of which 10 were waited for; matrix products, arithmetic and copies ran while one was open for 9% of the time, Pallas kernels for 0%

profile of v1, /device:TPU:0, one launch (start us, length us, event | category | flops | bytes accessed | tf_op | source)
XLA Modules:
  0.0 578.7 jit_solution(15166994795619813413)
XLA Ops:
  9.8 1.6 fusion.14
  11.8 1.3 fusion.6
  17.6 35.6 %all-gather.10.cloned.1.call-done.wout_ref = bf16[1024,512]{1,0:T(8,128)(2,1)} async-done(((bf16[128,512]{1,0:T(8,128)(2,1)}), bf16[1024,512]{1,0:T(8,128)(2,1)}) %all-gather.10.cloned.1.call-update) | async-done | bytes 1048592 | tf_op jit(solution)/shard_map/all_gather | solution.py:416
  53.2 58.8 %all-gather.8.cloned.1.call-done.w_ref = bf16[1024,1408]{1,0:T(8,128)(2,1)} async-done(((bf16[128,1408]{1,0:T(8,128)(2,1)}), bf16[1024,1408]{1,0:T(8,128)(2,1)}) %all-gather.8.cloned.1.call-update) | async-done | bytes 2883600 | tf_op jit(solution)/shard_map/all_gather | solution.py:415
  112.0 35.2 %all-gather.6.cloned.1.call-done.hid_ref = bf16[2048,1024]{1,0:T(8,128)(2,1)} async-done(((bf16[512,1024]{1,0:T(8,128)(2,1)}), bf16[2048,1024]{1,0:T(8,128)(2,1)}) %all-gather.6.cloned.1.call-update) | async-done | bytes 4194320 | tf_op jit(solution)/shard_map/all_gather | solution.py:420
  147.2 35.9 %all-gather.12.cloned.1.call-done = bf16[1,2048,1024]{2,1,0:T(8,128)(2,1)} async-done(((bf16[1,512,1024]{2,1,0:T(8,128)(2,1)}), bf16[1,2048,1024]{2,1,0:T(8,128)(2,1)}) %all-gather.12.cloned.1.call-update) | async-done | bytes 4194320 | tf_op jit(solution)/shard_map/all_gather | solution.py:423
  183.1 33.3 %mixer_forward.1 = (f32[2048,1408]{1,0:T(8,128)}, f32[2048,768]{1,0:T(8,128)}, f32[2048,512]{1,0:T(8,128)}, bf16[2048,512]{1,0:T(8,128)(2,1)}, f32[8,2048]{1,0:T(8,128)}, /*index=5*/bf16[16,512,128]{2,1,0:T(8,128)(2,1)}) custom-call(bf16[2048,1024]{1,0:T(8,128)(2,1)} %all-gather.6.cloned.1.call-done.hid_ref, ...), custom_call_target="tpu_custom_call" | custom-call | flops 9036103680 | bytes 32505856 | tf_op jit(solution)/shard_map/mixer_forward/pallas_call | solution.py:321
  216.5 31.6 %all-reduce.6.cloned.1.call-done.stat_ref = f32[8,2048]{1,0:T(8,128)} async-done(((f32[8,2048]{1,0:T(8,128)}), f32[8,2048]{1,0:T(8,128)}) %all-reduce.6.cloned.1.call-update) | async-done | bytes 65552 | tf_op jit(solution)/shard_map/psum | solution.py:445
  248.2 48.9 %mixer_backward.1 = (bf16[2048,512]{1,0:T(8,128)(2,1)}, bf16[2048,1408]{1,0:T(8,128)(2,1)}, f32[5,8,768]{2,1,0:T(8,128)}, f32[2,8,512]{2,1,0:T(8,128)}, f32[2,8,128]{2,1,0:T(8,128)}) custom-call(f32[2048,1408]{1,0:T(8,128)} %get-tuple-element.26.proj_ref, f32[2048,768]{1,0:T(8,128)} %get-tuple-element.27.pre_ref, f32[2048,512]{1,0:T(8,128)} %get-tuple-element.28.mixed_ref, ...), custom_call_target="tpu_custom_call" | custom-call | flops 3276800000 | bytes 31981568 | tf_op jit(solution)/shard_map/mixer_backward/pallas_call | solution.py:361
  297.1 3.9 fusion.11
  301.0 1.3 copy.39
  302.6 11.4 %convolution_convert_fusion = bf16[1024,1408]{1,0:T(8,128)(2,1)} fusion(bf16[2048,1024]{1,0:T(8,128)(2,1)} %all-gather.6.cloned.1.call-done.hid_ref, bf16[2048,1408]{1,0:T(8,128)(2,1)} %get-tuple-element.33), kind=kOutput, calls=%fused_computation.6 | convolution fusion | flops 5907021824 | bytes 12845056 | tf_op jit(solution)/shard_map/dot_general | solution.py:22
  314.1 11.5 %convolution_convert_fusion.1 = bf16[2048,1024]{1,0:T(8,128)(2,1)} fusion(bf16[2048,1408]{1,0:T(8,128)(2,1)} %get-tuple-element.33, bf16[1024,1408]{1,0:T(8,128)(2,1)} %all-gather.8.cloned.1.call-done.w_ref), kind=kOutput, calls=%fused_computation.7 | convolution fusion | flops 5907677184 | bytes 12845056 | tf_op jit(solution)/shard_map/dot_general | solution.py:22
  325.6 1.5 copy-done.15
  327.2 5.6 convolution_convert_fusion.2
  334.3 32.4 %reduce-scatter.13.cloned.1.call-done = bf16[128,512]{1,0:T(8,128)(2,1)} async-done(((bf16[1024,512]{1,0:T(8,128)(2,1)}), bf16[128,512]{1,0:T(8,128)(2,1)}) %reduce-scatter.13.cloned.1.call-update) | async-done | bytes 131088
  368.6 72.9 %reduce-scatter.11.cloned.1.call-done = bf16[128,1408]{1,0:T(8,128)(2,1)} async-done(((bf16[1024,1408]{1,0:T(8,128)(2,1)}), bf16[128,1408]{1,0:T(8,128)(2,1)}) %reduce-scatter.11.cloned.1.call-update) | async-done | bytes 360464 | tf_op jit(solution)/shard_map/reduce_scatter | solution.py:460
  445.2 42.7 %reduce-scatter.9.cloned.1.call-done = bf16[512,1024]{1,0:T(8,128)(2,1)} async-done(((bf16[2048,1024]{1,0:T(8,128)(2,1)}), bf16[512,1024]{1,0:T(8,128)(2,1)}) %reduce-scatter.9.cloned.1.call-update) | async-done | bytes 1048592 | tf_op jit(solution)/shard_map/reduce_scatter | solution.py:457
  487.9 2.2 fusion.10
  490.1 40.5 %psum.22 = f32[14688]{0:T(1024)S(1)} all-reduce(f32[14688]{0:T(1024)S(1)} %pad_maximum_fusion), channel_id=1, replica_groups=mesh['dp'=8,'tensor'=4] {'dp','tensor'}, use_global_device_ids=true, to_apply=%region_10.11 | all-reduce | flops 14688 | bytes 117504 | tf_op jit(solution)/shard_map/psum | solution.py:495
  531.8 4.0 reduce-scatter.7.cloned.1.call-done
  535.8 3.6 fusion.3
  541.8 28.5 %all-reduce.8.cloned.1.call-done = f32[128,256]{1,0:T(8,128)} async-done(((f32[128,256]{1,0:T(8,128)}), f32[128,256]{1,0:T(8,128)}) %all-reduce.8.cloned.1.call-update) | async-done | bytes 131088 | tf_op jit(solution)/shard_map/psum | solution.py:465
  570.3 1.6 copy.46
  (103 shorter events, 18.4 us)
Async XLA Ops:
  7.2 9.2 %copy-start = (f32[4,2048]{1,0:T(4,128)S(1)}, f32[4,2048]{1,0:T(4,128)}, u32[]{:S(2)}) copy-start(f32[4,2048]{1,0:T(4,128)} %param.22) | copy-start | bytes 98308
  7.2 4.3 copy-start.2
  7.2 4.6 copy-start.7
  7.2 46.0 %all-gather.10.cloned.1.call-start = ((), (), s32[]{:S(2)}) async-start(), calls=%async_computation.6 | async-start | bytes 1179648 | tf_op jit(solution)/shard_map/all_gather | solution.py:416
  8.0 104.0 %all-gather.8.cloned.1.call-start = ((), (), s32[]{:S(2)}) async-start(), calls=%async_computation.5 | async-start | bytes 3244032 | tf_op jit(solution)/shard_map/all_gather | solution.py:415
  11.4 135.8 %all-gather.6.cloned.1.call-start = ((), (), s32[]{:S(2)}) async-start(), calls=%async_computation.4 | async-start | bytes 5242880 | tf_op jit(solution)/shard_map/all_gather | solution.py:420
  11.8 2.8 copy-start.11
  11.8 3.5 copy-start.16
  11.8 3.8 copy-start.12
  11.8 3.8 copy-start.13
  11.8 5.1 copy-start.10
  13.1 170.0 %all-gather.12.cloned.1.call-start = ((), (), s32[]{:S(2)}) async-start(), calls=%async_computation.12 | async-start | bytes 5242880 | tf_op jit(solution)/shard_map/all_gather | solution.py:423
  13.7 234.4 %all-reduce.6.cloned.1.call-start = ((), (), s32[]{:S(2)}) async-start(), calls=%async_computation.7 | async-start | bytes 131072 | tf_op jit(solution)/shard_map/psum | solution.py:445
  216.5 150.3 %reduce-scatter.13.cloned.1.call-start = ((), (), s32[]{:S(2)}) async-start(), calls=%async_computation.13 | async-start | bytes 1179648
  248.2 48.9 %copy-start.14 = (bf16[1,2048,1024]{2,1,0:T(8,128)(2,1)S(1)}, bf16[1,2048,1024]{2,1,0:T(8,128)(2,1)}, u32[]{:S(2)}) copy-start(bf16[1,2048,1024]{2,1,0:T(8,128)(2,1)} %all-gather.12.cloned.1.call-done) | copy-start | bytes 12582916
  302.4 139.1 %reduce-scatter.11.cloned.1.call-start = ((), (), s32[]{:S(2)}) async-start(), calls=%async_computation.10 | async-start | bytes 3244032 | tf_op jit(solution)/shard_map/reduce_scatter | solution.py:460
  314.0 173.9 %reduce-scatter.9.cloned.1.call-start = ((), (), s32[]{:S(2)}) async-start(), calls=%async_computation.9 | async-start | bytes 5242880 | tf_op jit(solution)/shard_map/reduce_scatter | solution.py:457
  325.6 1.6 copy-start.15
  325.6 210.2 %reduce-scatter.7.cloned.1.call-start = ((), (), s32[]{:S(2)}) async-start(), calls=%async_computation.8 | async-start | bytes 5242880 | tf_op jit(solution)/shard_map/reduce_scatter | solution.py:450
  332.8 237.6 %all-reduce.8.cloned.1.call-start = ((), (), s32[]{:S(2)}) async-start(), calls=%async_computation.11 | async-start | bytes 262144 | tf_op jit(solution)/shard_map/psum | solution.py:465
  441.5 2.3 copy-start.5
  442.6 93.2 %copy-start.3 = (bf16[1,512,1024]{2,1,0:T(8,128)(2,1)S(1)}, bf16[1,512,1024]{2,1,0:T(8,128)(2,1)}, u32[]{:S(2)}) copy-start(bf16[1,512,1024]{2,1,0:T(8,128)(2,1)} %param.16) | copy-start | bytes 3145732
  487.9 47.9 %copy-start.4 = (bf16[512,1024]{1,0:T(8,128)(2,1)S(1)}, bf16[512,1024]{1,0:T(8,128)(2,1)}, u32[]{:S(2)}) copy-start(bf16[512,1024]{1,0:T(8,128)(2,1)} %reduce-scatter.9.cloned.1.call-done) | copy-start | bytes 3145732
  531.8 40.1 %copy-start.1 = (f32[4,2048]{1,0:T(4,128)S(1)}, f32[4,2048]{1,0:T(4,128)}, u32[]{:S(2)}) copy-start(f32[4,2048]{1,0:T(4,128)} %param.22) | copy-start | bytes 98308
  (3 other events, 3.1 us)
Sparse Core Ops, SparseCore 0:
  10.2 42.9 all-gather.9
  55.9 56.0 all-gather.7
  114.1 33.0 all-gather.5
  148.6 34.4 all-gather.11
  216.6 31.5 all-reduce.5
  302.5 64.1 reduce-scatter.12
  370.3 71.2 reduce-scatter.10
  444.1 43.8 reduce-scatter.8
  490.4 45.2 reduce-scatter.6
  538.5 31.7 all-reduce.7
